TPU v7x, 32 devices: a whole 2x2x4 slice. The times are simulated.
32 devices in a mesh: seq: 4 (over y, x), mem: 8 (over z, core).
Axes of the slice: x: 2, y: 2, z: 4, core: 2. Of those that a mesh axis runs over, the one named last changes fastest.
Arguments:
- hidden: bfloat16 [8192, 2048], P(('seq', 'mem')), may hold values from -6 to 6
- routes: int32 [8192, 2], P(('seq', 'mem')), may hold values from 0 to 7, all different within a row; in each aligned block of 256 rows (0 to 255, 256 to 511, ...) at most 64 rows name the same one
- gate_levels: int32 [8192, 2], P(('seq', 'mem')), may hold values from 1 to 255
- query_weight: bfloat16 [2048, 1024], P('seq'), may hold values from -0.125 to 0.125
- key_weight: bfloat16 [8, 2048, 1024], P('mem', 'seq'), may hold values from -0.125 to 0.125
- value_weight: bfloat16 [8, 2048, 1024], P('mem', 'seq'), may hold values from -0.125 to 0.125
Outputs:
- mixed: bfloat16 [8192, 1024], P(('seq', 'mem'))
Inputs may be any that keep to these rules, and one draw needn't show every extreme that they name: `routes`: the two memories of a row differ. In the rows of one device no memory is named by more than 64 rows, a bound that some block reaches.
All inputs are finite; a program needn't handle non-finite values.
Results may differ from a plain program's by a relative error of at most 0.01.
Values may be sent and summed in bfloat16 or wider, within the bound.
No kernel may reach another device: no remote copies, remote signals or barrier semaphores. Data moves between devices by JAX's collectives and lax.ppermute only.
A program may use at most 128 MiB of HBM per device.

v0:
```python
import jax
import jax.numpy as jnp
from jax import lax
from jax.sharding import PartitionSpec as P

HEADS = 8
DK = 128
BLOCK = 512
CAP = 64


def entering(array, axis, join, neutral):
    place = lax.axis_index(axis)
    gathered = lax.all_gather(array.astype(jnp.bfloat16), axis)
    state = jnp.zeros_like(array) + jnp.asarray(neutral, array.dtype)

    def one(step, state):
        return join(state, lax.dynamic_index_in_dim(gathered, step, 0, False).astype(array.dtype))

    return lax.fori_loop(0, place, one, state)


def add_states(earlier, later):
    return earlier + later


def on_device(hidden, routes, gate_levels, query_weight, key_weight, value_weight):
    count = hidden.shape[0]
    model = hidden.shape[1]
    width = query_weight.shape[1]
    mem_local = key_weight.shape[0]
    experts = mem_local * lax.axis_size("mem")
    highest = lax.Precision.HIGHEST
    onehot = (routes[:, :, None] == jnp.arange(experts, dtype=jnp.int32)[None, None, :]).astype(
        jnp.int32
    )
    per_token = jnp.sum(onehot, axis=1)
    before = jnp.cumsum(per_token, axis=0) - per_token
    place = jnp.sum(onehot * before[:, None, :], axis=2)
    slots = (routes * CAP + place).reshape(-1)
    owner_of = jnp.arange(2 * count, dtype=jnp.int32) // 2
    match = jnp.arange(experts * CAP, dtype=jnp.int32)[:, None] == slots[None, :]
    source = jnp.sum(jnp.where(match, owner_of[None, :], 0), axis=1)
    filled = jnp.any(match, axis=1)
    sent_rows = jnp.where(
        filled[:, None], jnp.take(hidden, source, axis=0), jnp.zeros((), hidden.dtype)
    )
    sent_rows = sent_rows.reshape(experts, CAP, model)
    columns = hidden
    queries = jnp.dot(
        columns,
        lax.all_gather(query_weight, "seq", axis=0, tiled=True),
        preferred_element_type=jnp.float32,
    ).astype(jnp.bfloat16)
    sent_queries = jnp.where(
        filled[:, None], jnp.take(queries, source, axis=0), jnp.zeros((), queries.dtype)
    )
    sent_queries = sent_queries.reshape(experts, CAP, width)
    arrived, arrived_queries = (
        lax.all_to_all(sent_rows, "mem", split_axis=0, concat_axis=1, tiled=True),
        lax.all_to_all(sent_queries, "mem", split_axis=0, concat_axis=1, tiled=True),
    )
    length = arrived.shape[1]
    columns = arrived
    key_part = jnp.einsum(
        "mrc,mch->mrh",
        columns,
        lax.all_gather(key_weight, "seq", axis=1, tiled=True),
        preferred_element_type=jnp.float32,
    )
    value_part = jnp.einsum(
        "mrc,mch->mrh",
        columns,
        lax.all_gather(value_weight, "seq", axis=1, tiled=True),
        preferred_element_type=jnp.float32,
    )
    keys = key_part
    values = value_part
    keys = keys.astype(jnp.bfloat16)
    values = values.astype(jnp.bfloat16)
    nblocks = length // BLOCK
    shape5 = (mem_local, nblocks, BLOCK, HEADS, DK)
    q_five = arrived_queries.reshape(shape5)
    k_five = keys.reshape(shape5)
    v_five = values.reshape(shape5)
    block_states = jnp.einsum(
        "mnkhd,mnkhe->mnhde", k_five, v_five, preferred_element_type=jnp.float32
    )
    within = jnp.cumsum(block_states, axis=1) - block_states
    local_total = jnp.sum(block_states, axis=1)
    nothing = jnp.zeros_like(local_total)
    incoming = entering(local_total, "seq", add_states, nothing)
    states = (incoming[:, None] + within).reshape(mem_local * nblocks, HEADS, DK, DK)
    flat = (mem_local * nblocks, BLOCK, HEADS, DK)
    rowids = jnp.arange(BLOCK, dtype=jnp.int32)
    causal = (rowids[:, None] >= rowids[None, :]).astype(jnp.float32)

    def attend(inputs):
        q_block, k_block, v_block, state = inputs
        scores = (
            jnp.einsum("qhd,khd->hqk", q_block, k_block, preferred_element_type=jnp.float32)
            * causal[None]
        )
        local = jnp.einsum("hqk,khd->qhd", scores, v_block.astype(jnp.float32), precision=highest)
        carried = jnp.einsum("qhd,hde->qhe", q_block.astype(jnp.float32), state, precision=highest)
        reads = local + carried
        scale = lax.rsqrt(jnp.mean(reads * reads, axis=-1, keepdims=True) + 1e-06)
        return (reads * scale).astype(jnp.bfloat16)

    normed = lax.map(
        attend, (q_five.reshape(flat), k_five.reshape(flat), v_five.reshape(flat), states)
    )
    normed = normed.reshape(mem_local, length, width)
    returned = lax.all_to_all(normed, "mem", split_axis=1, concat_axis=0, tiled=True)
    returned = returned.reshape(experts * CAP, width)
    picked = jnp.take(returned, slots, axis=0).reshape(count, 2, width)
    levels = gate_levels.astype(jnp.float32)
    gates = levels / jnp.sum(levels, axis=1, keepdims=True)
    mixed = jnp.sum(gates[:, :, None] * picked.astype(jnp.float32), axis=1)
    return mixed.astype(jnp.bfloat16)


def solution(mesh):
    return jax.shard_map(
        on_device,
        mesh=mesh,
        in_specs=(
            P(("seq", "mem"), None),
            P(("seq", "mem"), None),
            P(("seq", "mem"), None),
            P("seq", None),
            P("mem", "seq", None),
            P("mem", "seq", None),
        ),
        out_specs=P(("seq", "mem"), None),
        check_vma=False,
    )
```

profile of v0, /device:TPU:0, one launch (start us, length us, event | category | flops | bytes accessed | tf_op | source)
XLA Modules:
  0.0 289.7 jit_solution(13704537950358973058)
XLA Ops:
  10.6 2.5 gather_fusion
  13.5 55.2 %all_to_all.12 = bf16[8,64,2048]{2,1,0:T(8,128)(2,1)S(1)} all-to-all(bf16[8,64,2048]{2,1,0:T(8,128)(2,1)S(1)} %select_select_fusion), channel_id=1, replica_groups=mesh['seq'=4,'mem'=8] {'mem'}, dimensions={0} | all-to-all | bytes 4194304 | tf_op jit(solution)/shard_map/all_to_all | solution.py:60
  70.0 5.5 %fusion.15 = bf16[512,1024]{1,0:T(8,128)(2,1)} fusion(bf16[512,2048]{1,0:T(8,128)(2,1)S(1)} %bitcast.80, bf16[1,2048,1024]{2,1,0:T(8,128)(2,1)} %all-gather.10.cloned.1.call-done), kind=kOutput, calls=%fused_computation.20 | convolution fusion | flops 2148007936 | bytes 7340032 | tf_op jit(solution)/shard_map/mrc,mch->mrh/dot_general | solution.py:65
  75.5 1.6 copy.74
  77.1 41.9 %all-gather.6.cloned.1.call-done = bf16[1,2048,1024]{2,1,0:T(8,128)(2,1)} async-done(((bf16[1,512,1024]{2,1,0:T(8,128)(2,1)}), bf16[1,2048,1024]{2,1,0:T(8,128)(2,1)}) %all-gather.6.cloned.1.call-update) | async-done | bytes 4194320 | tf_op jit(solution)/shard_map/all_gather | solution.py:74
  119.0 5.2 %fusion.18 = bf16[64,8,8,128]{3,2,1,0:T(8,128)(2,1)S(1)} fusion(bf16[512,2048]{1,0:T(8,128)(2,1)} %bitcast.81, bf16[1,2048,1024]{2,1,0:T(8,128)(2,1)} %all-gather.6.cloned.1.call-done), kind=kOutput, calls=%fused_computation.21 | convolution fusion | flops 2148007936 | bytes 7340032 | tf_op jit(solution)/shard_map/mrc,mch->mrh/dot_general | solution.py:71
  126.3 47.1 %all-gather.8.cloned.1.call-done = bf16[2048,1024]{1,0:T(8,128)(2,1)} async-done(((bf16[512,1024]{1,0:T(8,128)(2,1)}), bf16[2048,1024]{1,0:T(8,128)(2,1)}) %all-gather.8.cloned.1.call-update) | async-done | bytes 4194320 | tf_op jit(solution)/shard_map/all_gather | solution.py:52
  173.5 3.4 %convolution_convert_fusion = bf16[256,1024]{1,0:T(8,128)(2,1)S(1)} fusion(bf16[256,2048]{1,0:T(8,128)(2,1)S(1)} %copy-done, bf16[2048,1024]{1,0:T(8,128)(2,1)} %all-gather.8.cloned.1.call-done), kind=kOutput, calls=%fused_computation.22 | convolution fusion | flops 1074003968 | bytes 5767168 | tf_op jit(solution)/shard_map/dot_general | solution.py:50
  176.9 2.8 gather_fusion.1
  179.7 2.4 select_select_fusion.1
  182.1 4.6 %all-to-all-start.1 = ((bf16[8,64,1024]{2,1,0:T(8,128)(2,1)}), bf16[8,64,1024]{2,1,0:T(8,128)(2,1)}, u32[]{:S(2)}, u32[]{:S(2)}) async-start(bf16[8,64,1024]{2,1,0:T(8,128)(2,1)} %select_select_fusion.1), calls=%async_computation.1 | async-start | bytes 2097152 | tf_op jit(solution)/shard_map/all_to_all | solution.py:61
  187.8 13.9 %all-gather.12.cloned.1.call-done = bf16[32,128,128]{2,1,0:T(8,128)(2,1)} async-done(((bf16[8,128,128]{2,1,0:T(8,128)(2,1)}), bf16[32,128,128]{2,1,0:T(8,128)(2,1)}) %all-gather.12.cloned.1.call-update) | async-done | bytes 1048592 | tf_op jit(solution)/shard_map/all_gather | solution.py:14
  201.9 11.5 %all-to-all-done.1 = bf16[8,64,1024]{2,1,0:T(8,128)(2,1)} async-done(((bf16[8,64,1024]{2,1,0:T(8,128)(2,1)}), bf16[8,64,1024]{2,1,0:T(8,128)(2,1)}, u32[]{:S(2)}, u32[]{:S(2)}) %all-to-all-start.1) | async-done | bytes 1048608 | tf_op jit(solution)/shard_map/all_to_all | solution.py:61
  213.4 1.5 copy.76
  217.7 5.5 %fusion.7 = (f32[512,8]{0,1:T(8,128)S(1)}, f32[8,128,512]{2,1,0:T(8,128)S(1)}) fusion(f32[8,128,512]{2,1,0:T(8,128)S(1)} %fusion.28, f32[8,512,512]{2,1,0:T(8,128)S(1)} %fusion.30, f32[512,512]{1,0:T(8,128)S(1)} %copy-done.1, bf16[64,8,8,128]{3,2,1,0:T(8,128)(2,1)S(1)} %copy-done.3), kind=kOutput, calls=%fused_computation.13 | convolution fusion | flops 3224891392 | bytes 14696448 | tf_op jit(solution)/shard_map/while/body/eval_jaxpr/hqk,khd->qhd/dot_general | solution.py:104
  224.5 4.7 %copy.70 = bf16[1,512,1024]{2,0,1:T(2,128)(2,1)S(1)} copy(bf16[1,512,1024]{1,2,0:T(8,128)(2,1)} %bitcast.78) | data formatting | bytes 2097152 | tf_op jit(solution)/shard_map/reshape | solution.py:113
  229.8 7.8 %reduce.2 = bf16[512,1024]{1,0:T(8,128)(2,1)} reduce(bf16[512,1,1024]{2,1,0:T(2,128)(2,1)S(1)} %bitcast.77, bf16[]{:T(256)} %broadcast.156), dimensions={1}, to_apply=%bitcast.55.reduce_sub_computation | reduce | bytes 2097154
  237.5 2.6 reshape.245
  240.2 3.6 %all-to-all-start.2 = ((bf16[8,2,32768]{2,1,0:T(2,128)(2,1)}), bf16[8,2,32768]{2,1,0:T(2,128)(2,1)S(1)}, u32[]{:S(2)}, u32[]{:S(2)}) async-start(bf16[8,2,32768]{2,1,0:T(2,128)(2,1)} %reshape.245), calls=%async_computation.2 | async-start | bytes 2097152 | tf_op jit(solution)/shard_map/all_to_all | solution.py:114
  244.3 26.0 %all-to-all-done.2 = bf16[8,2,32768]{2,1,0:T(2,128)(2,1)S(1)} async-done(((bf16[8,2,32768]{2,1,0:T(2,128)(2,1)}), bf16[8,2,32768]{2,1,0:T(2,128)(2,1)S(1)}, u32[]{:S(2)}, u32[]{:S(2)}) %all-to-all-start.2) | async-done | bytes 1048608 | tf_op jit(solution)/shard_map/all_to_all | solution.py:114
  270.2 3.5 %reshape.246 = bf16[512,1,1024]{2,1,0:T(2,128)(2,1)} reshape(bf16[8,2,32768]{2,1,0:T(2,128)(2,1)S(1)} %all-to-all-done.2) | data formatting | bytes 2097152
  273.7 2.0 copy.94
  275.6 2.1 gather_fusion.2
  278.2 5.0 %multiply_reduce_fusion = bf16[256,1024]{1,0:T(8,128)(2,1)} fusion(bf16[256,2,1024]{2,1,0:T(2,128)(2,1)S(1)} %gather.23, pred[256,2]{1,0:T(8,128)(4,1)S(1)} %copy.60, f32[256,2]{1,0:T(8,128)S(1)} %copy.59), kind=kLoop, calls=%fused_computation.15 | loop fusion | flops 1835008 | bytes 1575424 | tf_op jit(solution)/shard_map/reduce_sum | solution.py:119
  (59 shorter events, 14.7 us)
Async XLA Ops:
  6.5 4.1 %copy-start = (bf16[256,2048]{1,0:T(8,128)(2,1)S(1)}, bf16[256,2048]{1,0:T(8,128)(2,1)}, u32[]{:S(2)}) copy-start(bf16[256,2048]{1,0:T(8,128)(2,1)} %param.8) | copy-start | bytes 3145732
  6.5 2.3 copy-start.5
  6.5 62.1 %all-gather.10.cloned.1.call-start = ((), (), s32[]{:S(2)}) async-start(), calls=%async_computation.5 | async-start | bytes 5242880 | tf_op jit(solution)/shard_map/all_gather | solution.py:68
  7.3 111.8 %all-gather.6.cloned.1.call-start = ((), (), s32[]{:S(2)}) async-start(), calls=%async_computation.3 | async-start | bytes 5242880 | tf_op jit(solution)/shard_map/all_gather | solution.py:74
  8.0 165.5 %all-gather.8.cloned.1.call-start = ((), (), s32[]{:S(2)}) async-start(), calls=%async_computation.4 | async-start | bytes 5242880 | tf_op jit(solution)/shard_map/all_gather | solution.py:52
  8.7 193.0 %all-gather.12.cloned.1.call-start = ((), (), s32[]{:S(2)}) async-start(), calls=%async_computation.6 | async-start | bytes 1310720 | tf_op jit(solution)/shard_map/all_gather | solution.py:14
  68.7 1.4 copy-start.4
  124.2 1.0 copy-start.2
  182.1 31.3 %all-to-all-start.1 = ((bf16[8,64,1024]{2,1,0:T(8,128)(2,1)}), bf16[8,64,1024]{2,1,0:T(8,128)(2,1)}, u32[]{:S(2)}, u32[]{:S(2)}) async-start(bf16[8,64,1024]{2,1,0:T(8,128)(2,1)} %select_select_fusion.1), calls=%async_computation.1 | async-start | bytes 2097152 | tf_op jit(solution)/shard_map/all_to_all | solution.py:61
  216.1 1.2 copy-start.1
  216.2 1.5 copy-start.3
  237.5 6.5 %copy-start.6 = (s32[256,2]{0,1:T(2,128)S(1)}, s32[256,2]{0,1:T(2,128)}, u32[]{:S(2)}) copy-start(s32[256,2]{0,1:T(2,128)} %param.10) | copy-start | bytes 6148
  240.2 30.1 %all-to-all-start.2 = ((bf16[8,2,32768]{2,1,0:T(2,128)(2,1)}), bf16[8,2,32768]{2,1,0:T(2,128)(2,1)S(1)}, u32[]{:S(2)}, u32[]{:S(2)}) async-start(bf16[8,2,32768]{2,1,0:T(2,128)(2,1)} %reshape.245), calls=%async_computation.2 | async-start | bytes 2097152 | tf_op jit(solution)/shard_map/all_to_all | solution.py:114
Sparse Core Ops, SparseCore 0:
  9.2 55.3 all-gather.9
  66.4 52.5 all-gather.5
  120.9 52.5 all-gather.7
  175.2 26.4 all-gather.11
where the time goes:
time: 290 us
  waiting for transfers between devices  142 us (49%)
  blocking collectives  55.2 us (19%)
  local copies, waits for them, and re-layouts  28.1 us (10%)
  matrix products  23 us (8%)
  other arithmetic  19.1 us (7%)
  between operations  13.4 us (5%)
  starting transfers between devices  8.28 us (3%)
    all_to_all x1, blocking collectives, on_device(): lax.all_to_all(sent_rows, 'mem', split_axis=0, concat_axis=1, tiled=True)  55.2 us
    all_gather x1, waiting for transfers between devices, on_device(): lax.all_gather(query_weight, 'seq', axis=0, tiled=True)  47.1 us
    all_gather x1, waiting for transfers between devices, on_device(): lax.all_gather(value_weight, 'seq', axis=1, tiled=True)  41.9 us
    all_to_all x1, waiting for transfers between devices, on_device(): lax.all_to_all(normed, 'mem', split_axis=1, concat_axis=0, tiled=True)  26 us
    all_gather x1, waiting for transfers between devices, entering(): gathered = lax.all_gather(array.astype(jnp.bfloat16), axis)  13.9 us
    unnamed x19, local copies, waits for them, and re-layouts  12.9 us
    all_to_all x1, waiting for transfers between devices, on_device(): lax.all_to_all(sent_queries, 'mem', split_axis=0, concat_axis=1, tiled=True)  11.5 us
    unnamed x1, other arithmetic  7.77 us
  transfers between devices with their start and end apart: 6, of which 5 were waited for; matrix products, arithmetic and copies ran while one was open for 10% of the time, Pallas kernels for 0%

commit v1 on v0

--- a/solution.py
+++ b/solution.py
@@ -68,12 +68,22 @@
         lax.all_gather(key_weight, "seq", axis=1, tiled=True),
         preferred_element_type=jnp.float32,
     )
-    value_part = jnp.einsum(
-        "mrc,mch->mrh",
-        columns,
-        lax.all_gather(value_weight, "seq", axis=1, tiled=True),
-        preferred_element_type=jnp.float32,
-    )
+    count_2, index, extent = (lax.axis_size("seq"), lax.axis_index("seq"), value_weight.shape[1])
+    upward = [(i, (i + 1) % count_2) for i in range(count_2)]
+    held, so_far = (value_weight, None)
+    for step_2 in range(count_2):
+        arriving = lax.ppermute(held, "seq", upward) if step_2 < count_2 - 1 else None
+        update = jnp.einsum(
+            "mrc,mch->mrh",
+            lax.dynamic_slice_in_dim(
+                columns, (index - step_2) % count_2 * extent, held.shape[1], axis=2
+            ),
+            held,
+            preferred_element_type=jnp.float32,
+        )
+        so_far = update if so_far is None else so_far + update
+        held = arriving
+    value_part = so_far
     keys = key_part
     values = value_part
     keys = keys.astype(jnp.bfloat16)

time: 290 us -> 279 us (0.962)
  blocking collectives: 55.2 us -> 0 us
  waiting for transfers between devices: 142 us -> 175 us
  starting transfers between devices: 8.28 us -> 16 us
  matrix products: 23 us -> 26.5 us
    ppermute x0 -> x3, waiting for transfers between devices: none -> 114 us  [on_device(): lax.ppermute(held, 'seq', upward)]
    all_to_all x1 -> x0, blocking collectives: 55.2 us -> none  [on_device(): lax.all_to_all(sent_rows, 'mem', split_axis=0, concat_axis=1, tiled=True)]
    all_gather x1 -> x0, waiting for transfers between devices: 41.9 us -> none  [on_device(): lax.all_gather(value_weight, 'seq', axis=1, tiled=True)]
    all_gather x1, waiting for transfers between devices: 47.1 us -> 7.64 us  [on_device(): lax.all_gather(query_weight, 'seq', axis=0, tiled=True)]
    all_to_all x0 -> x1, starting transfers between devices: none -> 6.35 us  [on_device(): lax.all_to_all(sent_rows, 'mem', split_axis=0, concat_axis=1, tiled=True)]
    dot_general x1 -> x4, matrix products: 5.15 us -> 7.7 us  [on_device(): jnp.einsum('mrc,mch->mrh', lax.dynamic_slice_in_dim(columns, (index - ste...]
    unnamed x19 -> x25, local copies, waits for them, and re-layouts: 12.9 us -> 11.3 us
  transfers between devices with their start and end apart: 6 -> 9, of which waited for: 5 -> 7; matrix products, arithmetic and copies ran while one was open for 10% -> 12% of each run, Pallas kernels for 0% -> 0%
where the time goes in v1:
time: 279 us; the launch traced here: 278 us
  waiting for transfers between devices  175 us (63%)
  matrix products  26.5 us (9%)
  local copies, waits for them, and re-layouts  26.4 us (9%)
  other arithmetic  20.5 us (7%)
  starting transfers between devices  16 us (6%)
  between operations  13.4 us (5%)
    ppermute x3, waiting for transfers between devices, on_device(): lax.ppermute(held, 'seq', upward)  114 us
    all_to_all x1, waiting for transfers between devices, on_device(): lax.all_to_all(normed, 'mem', split_axis=1, concat_axis=0, tiled=True)  26 us
    all_gather x1, waiting for transfers between devices, entering(): gathered = lax.all_gather(array.astype(jnp.bfloat16), axis)  13.1 us
    all_to_all x1, waiting for transfers between devices, on_device(): lax.all_to_all(sent_queries, 'mem', split_axis=0, concat_axis=1, tiled=True)  12.2 us
    unnamed x25, local copies, waits for them, and re-layouts  11.3 us
    unnamed x1, other arithmetic  7.77 us
    dot_general x4, matrix products, on_device(): jnp.einsum('mrc,mch->mrh', lax.dynamic_slice_in_dim(columns, (index - ste...  7.7 us
    all_gather x1, waiting for transfers between devices, on_device(): lax.all_gather(query_weight, 'seq', axis=0, tiled=True)  7.64 us
  transfers between devices with their start and end apart: 9, of which 7 were waited for; matrix products, arithmetic and copies ran while one was open for 12% of the time, Pallas kernels for 0%

profile of v1, /device:TPU:0, one launch (start us, length us, event | category | flops | bytes accessed | tf_op | source)
XLA Modules:
  0.0 277.9 jit_solution(11679175340468570167)
XLA Ops:
  9.9 2.5 gather_fusion
  14.1 6.4 %all-to-all-start = ((bf16[8,64,2048]{2,1,0:T(8,128)(2,1)}), bf16[8,64,2048]{2,1,0:T(8,128)(2,1)S(1)}, u32[]{:S(2)}, u32[]{:S(2)}) async-start(bf16[8,64,2048]{2,1,0:T(8,128)(2,1)} %select_select_fusion), calls=%async_computation | async-start | bytes 4194304 | tf_op jit(solution)/shard_map/all_to_all | solution.py:60
  22.0 40.1 %collective-permute-done = bf16[1,512,1024]{2,1,0:T(8,128)(2,1)S(1)} collective-permute-done((bf16[1,512,1024]{2,1,0:T(8,128)(2,1)}, bf16[1,512,1024]{2,1,0:T(8,128)(2,1)S(1)}, u32[]{:S(2)}, u32[]{:S(2)}) %collective-permute-start) | collective-permute-done | bytes 1048608 | tf_op jit(solution)/shard_map/ppermute | solution.py:75
  63.1 38.9 %collective-permute-done.1 = bf16[1,512,1024]{2,1,0:T(8,128)(2,1)} collective-permute-done((bf16[1,512,1024]{2,1,0:T(8,128)(2,1)S(1)}, bf16[1,512,1024]{2,1,0:T(8,128)(2,1)}, u32[]{:S(2)}, u32[]{:S(2)}) %collective-permute-start.1) | collective-permute-done | bytes 1048608 | tf_op jit(solution)/shard_map/ppermute | solution.py:75
  102.1 2.8 fusion.22
  107.6 35.4 %collective-permute-done.2 = bf16[1,512,1024]{2,1,0:T(8,128)(2,1)} collective-permute-done((bf16[1,512,1024]{2,1,0:T(8,128)(2,1)}, bf16[1,512,1024]{2,1,0:T(8,128)(2,1)}, u32[]{:S(2)}, u32[]{:S(2)}) %collective-permute-start.2) | collective-permute-done | bytes 1048608 | tf_op jit(solution)/shard_map/ppermute | solution.py:75
  143.0 2.2 fusion.13
  145.2 6.1 %fusion.10 = bf16[512,1024]{1,0:T(8,128)(2,1)} fusion(bf16[512,2048]{1,0:T(8,128)(2,1)} %bitcast.98, bf16[1,2048,1024]{2,1,0:T(8,128)(2,1)} %all-gather.7.cloned.1.call-done), kind=kOutput, calls=%fused_computation.18 | convolution fusion | flops 2148007936 | bytes 7340032 | tf_op jit(solution)/shard_map/mrc,mch->mrh/dot_general | solution.py:65
  154.3 7.6 %all-gather.5.cloned.1.call-done = bf16[2048,1024]{1,0:T(8,128)(2,1)} async-done(((bf16[512,1024]{1,0:T(8,128)(2,1)}), bf16[2048,1024]{1,0:T(8,128)(2,1)}) %all-gather.5.cloned.1.call-update) | async-done | bytes 4194320 | tf_op jit(solution)/shard_map/all_gather | solution.py:52
  161.9 3.4 %convolution_convert_fusion = bf16[256,1024]{1,0:T(8,128)(2,1)S(1)} fusion(bf16[256,2048]{1,0:T(8,128)(2,1)S(1)} %copy-done, bf16[2048,1024]{1,0:T(8,128)(2,1)} %all-gather.5.cloned.1.call-done), kind=kOutput, calls=%fused_computation.20 | convolution fusion | flops 1074003968 | bytes 5767168 | tf_op jit(solution)/shard_map/dot_general | solution.py:50
  165.3 2.8 %gather_fusion.1 = bf16[512,1024]{1,0:T(8,128)(2,1)} fusion(bf16[256,1024]{1,0:T(8,128)(2,1)S(1)} %convolution_convert_fusion, s32[1024]{0:T(1024)S(1)} %pad_clamp_fusion.1), kind=kCustom, calls=%fused_computation.1 | custom fusion | bytes 2099200 | tf_op jit(solution)/shard_map/jit(_take)/gather | solution.py:56
  168.1 2.5 select_select_fusion.1
  170.6 4.5 %all-to-all-start.1 = ((bf16[8,64,1024]{2,1,0:T(8,128)(2,1)}), bf16[8,64,1024]{2,1,0:T(8,128)(2,1)}, u32[]{:S(2)}, u32[]{:S(2)}) async-start(bf16[8,64,1024]{2,1,0:T(8,128)(2,1)} %select_select_fusion.1), calls=%async_computation.1 | async-start | bytes 2097152 | tf_op jit(solution)/shard_map/all_to_all | solution.py:61
  176.2 13.1 %all-gather.9.cloned.1.call-done = bf16[32,128,128]{2,1,0:T(8,128)(2,1)} async-done(((bf16[8,128,128]{2,1,0:T(8,128)(2,1)}), bf16[32,128,128]{2,1,0:T(8,128)(2,1)}) %all-gather.9.cloned.1.call-update) | async-done | bytes 1048592 | tf_op jit(solution)/shard_map/all_gather | solution.py:14
  189.6 12.2 %all-to-all-done.1 = bf16[8,64,1024]{2,1,0:T(8,128)(2,1)} async-done(((bf16[8,64,1024]{2,1,0:T(8,128)(2,1)}), bf16[8,64,1024]{2,1,0:T(8,128)(2,1)}, u32[]{:S(2)}, u32[]{:S(2)}) %all-to-all-start.1) | async-done | bytes 1048608 | tf_op jit(solution)/shard_map/all_to_all | solution.py:61
  205.8 5.5 %fusion.5 = (f32[512,8]{0,1:T(8,128)S(1)}, f32[8,128,512]{2,1,0:T(8,128)S(1)}) fusion(f32[8,128,512]{2,1,0:T(8,128)S(1)} %fusion.28, f32[8,512,512]{2,1,0:T(8,128)S(1)} %fusion.30, f32[512,512]{1,0:T(8,128)S(1)} %copy-done.4, bf16[64,8,8,128]{3,2,1,0:T(8,128)(2,1)S(1)} %fusion.13), kind=kOutput, calls=%fused_computation.11 | convolution fusion | flops 3224891392 | bytes 14696448 | tf_op jit(solution)/shard_map/while/body/eval_jaxpr/hqk,khd->qhd/dot_general | solution.py:114
  212.7 4.7 %copy.70 = bf16[1,512,1024]{2,0,1:T(2,128)(2,1)S(1)} copy(bf16[1,512,1024]{1,2,0:T(8,128)(2,1)} %bitcast.100) | data formatting | bytes 2097152 | tf_op jit(solution)/shard_map/reshape | solution.py:123
  217.9 7.8 %reduce.2 = bf16[512,1024]{1,0:T(8,128)(2,1)} reduce(bf16[512,1,1024]{2,1,0:T(2,128)(2,1)S(1)} %bitcast.99, bf16[]{:T(256)} %broadcast.164), dimensions={1}, to_apply=%bitcast.73.reduce_sub_computation | reduce | bytes 2097154
  225.7 2.6 reshape.277
  228.4 3.6 %all-to-all-start.2 = ((bf16[8,2,32768]{2,1,0:T(2,128)(2,1)}), bf16[8,2,32768]{2,1,0:T(2,128)(2,1)S(1)}, u32[]{:S(2)}, u32[]{:S(2)}) async-start(bf16[8,2,32768]{2,1,0:T(2,128)(2,1)} %reshape.277), calls=%async_computation.2 | async-start | bytes 2097152 | tf_op jit(solution)/shard_map/all_to_all | solution.py:124
  232.5 26.0 %all-to-all-done.2 = bf16[8,2,32768]{2,1,0:T(2,128)(2,1)S(1)} async-done(((bf16[8,2,32768]{2,1,0:T(2,128)(2,1)}), bf16[8,2,32768]{2,1,0:T(2,128)(2,1)S(1)}, u32[]{:S(2)}, u32[]{:S(2)}) %all-to-all-start.2) | async-done | bytes 1048608 | tf_op jit(solution)/shard_map/all_to_all | solution.py:124
  258.4 3.5 %reshape.278 = bf16[512,1,1024]{2,1,0:T(2,128)(2,1)} reshape(bf16[8,2,32768]{2,1,0:T(2,128)(2,1)S(1)} %all-to-all-done.2) | data formatting | bytes 2097152
  263.8 2.1 gather_fusion.2
  266.4 5.0 %multiply_reduce_fusion = bf16[256,1024]{1,0:T(8,128)(2,1)} fusion(bf16[256,2,1024]{2,1,0:T(2,128)(2,1)S(1)} %gather.23, pred[256,2]{1,0:T(8,128)(4,1)S(1)} %copy.60, f32[256,2]{1,0:T(8,128)S(1)} %copy.59), kind=kLoop, calls=%fused_computation.13 | loop fusion | flops 1835008 | bytes 1575424 | tf_op jit(solution)/shard_map/reduce_sum | solution.py:129
  (72 shorter events, 23.3 us)
Async XLA Ops:
  6.5 3.3 %copy-start = (bf16[256,2048]{1,0:T(8,128)(2,1)S(1)}, bf16[256,2048]{1,0:T(8,128)(2,1)}, u32[]{:S(2)}) copy-start(bf16[256,2048]{1,0:T(8,128)(2,1)} %param.8) | copy-start | bytes 3145732
  6.5 1.5 copy-start.8
  6.5 138.7 %all-gather.7.cloned.1.call-start = ((), (), s32[]{:S(2)}) async-start(), calls=%async_computation.4 | async-start | bytes 5242880 | tf_op jit(solution)/shard_map/all_gather | solution.py:68
  7.3 154.6 %all-gather.5.cloned.1.call-start = ((), (), s32[]{:S(2)}) async-start(), calls=%async_computation.3 | async-start | bytes 5242880 | tf_op jit(solution)/shard_map/all_gather | solution.py:52
  14.1 88.0 %all-to-all-start = ((bf16[8,64,2048]{2,1,0:T(8,128)(2,1)}), bf16[8,64,2048]{2,1,0:T(8,128)(2,1)S(1)}, u32[]{:S(2)}, u32[]{:S(2)}) async-start(bf16[8,64,2048]{2,1,0:T(8,128)(2,1)} %select_select_fusion), calls=%async_computation | async-start | bytes 4194304 | tf_op jit(solution)/shard_map/all_to_all | solution.py:60
  20.4 168.9 %all-gather.9.cloned.1.call-start = ((), (), s32[]{:S(2)}) async-start(), calls=%async_computation.5 | async-start | bytes 1310720 | tf_op jit(solution)/shard_map/all_gather | solution.py:14
  20.5 41.7 %collective-permute-start = (bf16[1,512,1024]{2,1,0:T(8,128)(2,1)}, bf16[1,512,1024]{2,1,0:T(8,128)(2,1)S(1)}, u32[]{:S(2)}, u32[]{:S(2)}) collective-permute-start(bf16[1,512,1024]{2,1,0:T(8,128)(2,1)} %param.13), channel_id=1, source_target_pairs={{0,8},{8,16},{16,24},{24,0},{1,9},{9,17},{17,25},{25,1},{2,10},{10... | collective-permute-start | bytes 3145736 | tf_op jit(solution)/shard_map/ppermute | solution.py:75
  62.1 1.0 copy-start.6
  63.1 38.9 %collective-permute-start.1 = (bf16[1,512,1024]{2,1,0:T(8,128)(2,1)S(1)}, bf16[1,512,1024]{2,1,0:T(8,128)(2,1)}, u32[]{:S(2)}, u32[]{:S(2)}) collective-permute-start(bf16[1,512,1024]{2,1,0:T(8,128)(2,1)S(1)} %collective-permute-done), channel_id=1, source_target_pairs={{0,8},{8,16},{16,24},{24,0},{1,9},{9,17},{17,25},{25,1},{2,10},{10... | collective-permute-start | bytes 3145736 | tf_op jit(solution)/shard_map/ppermute | solution.py:75
  102.0 40.9 %collective-permute-start.2 = (bf16[1,512,1024]{2,1,0:T(8,128)(2,1)}, bf16[1,512,1024]{2,1,0:T(8,128)(2,1)}, u32[]{:S(2)}, u32[]{:S(2)}) collective-permute-start(bf16[1,512,1024]{2,1,0:T(8,128)(2,1)} %collective-permute-done.1), channel_id=1, source_target_pairs={{0,8},{8,16},{16,24},{24,0},{1,9},{9,17},{17,25},{25,1},{2,10},{10... | collective-permute-start | bytes 3145736 | tf_op jit(solution)/shard_map/ppermute | solution.py:75
  102.1 4.8 %copy-start.3 = (bf16[8,64,2048]{2,1,0:T(8,128)(2,1)}, bf16[8,64,2048]{2,1,0:T(8,128)(2,1)S(1)}, u32[]{:S(2)}) copy-start(bf16[8,64,2048]{2,1,0:T(8,128)(2,1)S(1)} %all-to-all-done) | copy-start | bytes 6291460
  104.8 2.1 copy-start.7
  152.8 1.4 copy-start.1
  170.6 31.2 %all-to-all-start.1 = ((bf16[8,64,1024]{2,1,0:T(8,128)(2,1)}), bf16[8,64,1024]{2,1,0:T(8,128)(2,1)}, u32[]{:S(2)}, u32[]{:S(2)}) async-start(bf16[8,64,1024]{2,1,0:T(8,128)(2,1)} %select_select_fusion.1), calls=%async_computation.1 | async-start | bytes 2097152 | tf_op jit(solution)/shard_map/all_to_all | solution.py:61
  201.8 1.6 copy-start.2
  203.3 1.3 copy-start.5
  204.6 1.2 copy-start.4
  225.7 6.5 %copy-start.9 = (s32[256,2]{0,1:T(2,128)S(1)}, s32[256,2]{0,1:T(2,128)}, u32[]{:S(2)}) copy-start(s32[256,2]{0,1:T(2,128)} %param.10) | copy-start | bytes 6148
  228.4 30.1 %all-to-all-start.2 = ((bf16[8,2,32768]{2,1,0:T(2,128)(2,1)}), bf16[8,2,32768]{2,1,0:T(2,128)(2,1)S(1)}, u32[]{:S(2)}, u32[]{:S(2)}) async-start(bf16[8,2,32768]{2,1,0:T(2,128)(2,1)} %reshape.277), calls=%async_computation.2 | async-start | bytes 2097152 | tf_op jit(solution)/shard_map/all_to_all | solution.py:124
Sparse Core Ops, SparseCore 0:
  9.2 83.3 all-gather.6
  94.4 67.4 all-gather.4
  163.7 25.5 all-gather.8
